TPU v7x, 128 devices: a whole 4x4x4 slice. The times are simulated.
128 devices in a mesh: row: 4 (over z), col: 2 (over y_lo), ex: 16 (over x, y_hi, core).
Axes of the slice: x: 4, y: 4 (y_hi: 2, y_lo: 2; y = y_hi * 2 + y_lo), z: 4, core: 2. Of those that a mesh axis runs over, the one named last changes fastest.
Arguments:
- train_in: bfloat16 [8192, 8192], P('ex', 'row'), may hold values from -6 to 6
- train_out: bfloat16 [8192, 8192], P('ex', 'col'), may hold values from -0.0047912598 to 0.0047912598
- query_in: bfloat16 [512, 8192], P('ex', 'row'), may hold values from -6 to 6
- query_out: bfloat16 [512, 8192], P('ex', 'col'), may hold values from -0.023925781 to 0.023925781
- query_ids: int32 [512], P('ex'), may hold values from 0 to 1
- in_basis: bfloat16 [8, 1024, 1024], P('row'), may hold values from -1 to 1, as said below
- out_basis: bfloat16 [8, 1024, 1024], P('col'), may hold values from -1 to 1, as said below
- level_table: float32 [64, 64], replicated, may hold values from 0.5 to 8
- in_level: int32 [8192], P('row'), may hold values from 0 to 63
- out_level: int32 [8192], P('col'), may hold values from 0 to 63
- lengths: int32 [4], replicated, may hold values from 1 to 4096, 8192 in all
Outputs:
- token_scores: float32 [2, 8192], P(None, 'ex')
- example_scores: float32 [2, 4], replicated
Inputs may be any that keep to these rules, and one draw needn't show every extreme that they name: `in_basis`: each block is an orthogonal matrix rounded to bfloat16. `out_basis`: each block is an orthogonal matrix rounded to bfloat16. `lengths`: the counts sum to 8192.
All inputs are finite; a program needn't handle non-finite values.
Results may differ from a plain program's by a relative error of at most 0.018.
Values may be sent and summed in bfloat16 or wider, within the bound.
No kernel may reach another device: no remote copies, remote signals or barrier semaphores. Data moves between devices by JAX's collectives and lax.ppermute only.
A program may use at most 192 MiB of HBM per device.

v0:
```python
import math
import jax
import jax.numpy as jnp
from jax import lax
from jax.sharding import PartitionSpec as P

QUERIES = 2
DAMPING = 0.1


def sent_together(arrays, axis, dim, along):
    widths = [math.prod(a.shape[along:]) for a in arrays]
    both = jnp.concatenate(
        [a.reshape(*a.shape[:along], w) for a, w in zip(arrays, widths)], axis=along
    )
    whole = lax.all_gather(both, axis, axis=dim, tiled=True)
    parts = jnp.split(whole, [sum(widths[:k]) for k in range(1, len(widths))], axis=along)
    return tuple((b.reshape(*whole.shape[:along], *a.shape[along:]) for a, b in zip(arrays, parts)))


def sent_to_all(shard, axis):
    size = lax.axis_size(axis)
    return lax.all_to_all(
        jnp.broadcast_to(shard[None], (size, *shard.shape)), axis, 0, 0, tiled=True
    )


def taken_together(shard, axis):
    everything = sent_to_all(shard, axis)
    return jnp.sum(everything, axis=0)


def body(
    train_in,
    train_out,
    query_in,
    query_out,
    query_ids,
    in_basis,
    out_basis,
    level_table,
    in_level,
    out_level,
    lengths,
):
    highest = lax.Precision.HIGHEST
    ex_count = lax.axis_size("ex")
    ex_index = lax.axis_index("ex")
    in_sub = in_basis.shape[0]
    out_sub = out_basis.shape[0]
    width = in_basis.shape[1]
    per_query = in_sub * out_sub
    owned = QUERIES * per_query // ex_count
    block_ids = ex_index * owned + jnp.arange(owned, dtype=jnp.int32)
    query_of = block_ids % QUERIES
    pair_of = block_ids // QUERIES
    out_of = pair_of // in_sub
    in_of = pair_of % in_sub
    out_own = jnp.take(out_basis, out_of, axis=0)
    in_own = jnp.take(in_basis, in_of, axis=0)
    query_code = query_of.astype(jnp.float32)
    piece_in, piece_out, piece_ids = sent_together(
        (query_in, query_out, query_ids.astype(jnp.bfloat16)), "ex", 0, 1
    )
    count = piece_in.shape[0]
    chosen_in = jnp.take(piece_in.reshape(count, in_sub, width), in_of, axis=1)
    chosen_out = jnp.take(piece_out.reshape(count, out_sub, width), out_of, axis=1)
    weights = (piece_ids.astype(jnp.float32)[:, None] == query_code[None, :]).astype(jnp.bfloat16)
    chosen_out = chosen_out * weights[:, :, None]
    grad_own = jnp.einsum("mka,mkb->kab", chosen_out, chosen_in, preferred_element_type=jnp.float32)
    grad_own = grad_own.astype(jnp.bfloat16)
    half = jnp.einsum("kab,kac->kbc", out_own, grad_own, preferred_element_type=jnp.float32).astype(
        jnp.bfloat16
    )
    rotated = jnp.einsum("kbc,kcd->kbd", half, in_own, preferred_element_type=jnp.float32)
    levels = jnp.arange(level_table.shape[0], dtype=jnp.int32)
    out_levels = jnp.take(out_level.reshape(out_sub, width), out_of, axis=0)
    in_levels = jnp.take(in_level.reshape(in_sub, width), in_of, axis=0)
    out_onehot = (out_levels[:, :, None] == levels[None, None, :]).astype(jnp.float32)
    in_onehot = (in_levels[:, :, None] == levels[None, None, :]).astype(jnp.float32)
    partway = jnp.einsum("kbl,lm->kbm", out_onehot, level_table, precision=highest)
    eigen = jnp.einsum("kbm,kdm->kbd", partway, in_onehot, precision=highest)
    damped = (rotated / (eigen + DAMPING)).astype(jnp.bfloat16)
    back = jnp.einsum("kbd,kcd->kbc", damped, in_own, preferred_element_type=jnp.float32).astype(
        jnp.bfloat16
    )
    precond = jnp.einsum("kab,kbc->kac", out_own, back, preferred_element_type=jnp.float32).astype(
        jnp.bfloat16
    )
    tokens = train_in.shape[0]
    in_split = train_in.reshape(tokens, in_sub, width)
    out_split = train_out.reshape(tokens, out_sub, width)
    query_range = jnp.arange(QUERIES, dtype=jnp.int32)
    piece = lax.all_gather(precond, "ex", axis=0, tiled=True)

    def score_one(step, running):
        pair = step // QUERIES
        matrix = lax.dynamic_index_in_dim(piece, step, 0, keepdims=False)
        acts = lax.dynamic_index_in_dim(in_split, pair % in_sub, 1, keepdims=False)
        grads = lax.dynamic_index_in_dim(out_split, pair // in_sub, 1, keepdims=False)
        image = lax.dot_general(
            acts, matrix, (((1,), (1,)), ((), ())), preferred_element_type=jnp.float32
        )
        values = jnp.sum(image * grads.astype(jnp.float32), axis=1)
        selector = (query_range == step % QUERIES).astype(jnp.float32)
        return running + selector[:, None] * values[None, :]

    token_part = lax.fori_loop(
        0, piece.shape[0], score_one, jnp.zeros((QUERIES, tokens), jnp.float32)
    )
    token_scores = taken_together(token_part, ("row", "col"))
    ends = jnp.cumsum(lengths)
    starts = ends - lengths
    positions = ex_index * tokens + jnp.arange(tokens, dtype=jnp.int32)
    member = (
        (positions[None, :] >= starts[:, None]) & (positions[None, :] < ends[:, None])
    ).astype(jnp.float32)
    local_part = lax.dot_general(token_scores, member, (((1,), (1,)), ((), ())), precision=highest)
    example_scores = taken_together(local_part, "ex")
    return (token_scores, example_scores)


def solution(mesh):
    placed = (
        P("ex", "row"),
        P("ex", "col"),
        P("ex", "row"),
        P("ex", "col"),
        P("ex"),
        P("row", None, None),
        P("col", None, None),
        P(),
        P("row"),
        P("col"),
        P(),
    )
    return jax.shard_map(
        body, mesh=mesh, in_specs=placed, out_specs=(P(None, "ex"), P()), check_vma=False
    )
```

profile of v0, /device:TPU:1, one launch (start us, length us, event | category | flops | bytes accessed | tf_op | source)
XLA Modules:
  0.0 416.8 jit_solution(11040072974099691769)
XLA Ops:
  11.9 66.4 %all-gather.4.cloned.1.call-done = bf16[512,6145]{1,0:T(8,128)(2,1)} async-done(((bf16[32,6145]{1,0:T(8,128)(2,1)}), bf16[512,6145]{1,0:T(8,128)(2,1)}) %all-gather.4.cloned.1.call-update) | async-done | bytes 6292496 | tf_op jit(solution)/shard_map/all_gather | solution.py:16
  78.3 4.7 %split.12 = bf16[512,4096]{1,0:T(8,128)(2,1)} slice(bf16[512,6145]{1,0:T(8,128)(2,1)} %all-gather.4.cloned.1.call-done), slice={[0:512], [2048:6144]} | slice | bytes 8388608 | tf_op jit(solution)/shard_map/split | solution.py:17
  83.0 6.5 %copy.58 = bf16[512,4096]{0,1:T(8,128)(2,1)} copy(bf16[512,4096]{1,0:T(8,128)(2,1)} %split.12) | data formatting | bytes 8388608
  96.5 5.5 %fusion.17 = bf16[1024,1024]{1,0:T(8,128)(2,1)S(1)} fusion(bf16[4,1024,1024]{2,1,0:T(8,128)(2,1)} %param.19, s32[]{:T(128)} %bitcast.3, pred[]{:T(512)} %bitcast.2, bf16[512,1,1024]{2,0,1:T(8,128)(2,1)S(1)} %copy.46, bf16[512,2,1024]{0,2,1:T(8,128)(2,1)} %bitcast.75, s32[]{:T(128)} %bitcast.12, pred[]{:T(512)} %bitcast.10, bf16[512]{0:T(512)(128)(2,1)S(1)} %fusion.55), kind=kOutput, calls=%fused_computation.19 | convolution fusion | flops 3224371200 | bytes 6294528 | tf_op jit(solution)/shard_map/kab,kac->kbc/dot_general | solution.py:72
  102.1 3.9 fusion.13
  108.5 8.1 %fusion.22 = bf16[1024,1024]{1,0:T(8,128)(2,1)} fusion(bf16[4,1024,1024]{2,1,0:T(8,128)(2,1)} %param.19, s32[]{:T(128)} %bitcast.3, pred[]{:T(512)} %bitcast.2, bf16[1024,1024]{1,0:T(8,128)(2,1)S(1)} %divide_convert_fusion, bf16[2,1024,1024]{2,1,0:T(8,128)(2,1)} %param.18, s32[]{:T(128)} %bitcast.12, pred[]{:T(512)} %bitcast.10), kind=kOutput, calls=%fused_computation.26 | convolution fusion | flops 4299161600 | bytes 8390656 | tf_op jit(solution)/shard_map/kab,kbc->kac/dot_general | solution.py:87
  116.6 6.7 %copy.49 = bf16[512,4096]{0,1:T(8,128)(2,1)} copy(bf16[512,4096]{1,0:T(8,128)(2,1)} %param.14) | data formatting | bytes 8388608 | tf_op args[1]
  126.1 176.4 %all-gather.6.cloned.1.call-done = bf16[16384,1024]{1,0:T(8,128)(2,1)} async-done(((bf16[1024,1024]{1,0:T(8,128)(2,1)}), bf16[16384,1024]{1,0:T(8,128)(2,1)}) %all-gather.6.cloned.1.call-update) | async-done | bytes 33554448 | tf_op jit(solution)/shard_map/all_gather | solution.py:94
  302.5 84.1 %while.23 = (s32[]{:T(128)}, f32[2,512]{1,0:T(2,128)S(1)}, bf16[512,2,1024]{0,2,1:T(8,128)(2,1)}, bf16[16,1024,1024]{2,1,0:T(8,128)(2,1)}, bf16[512,4,1024]{0,2,...) while((s32[]{:T(128)}, f32[2,512]{1,0:T(2,128)S(1)}, ...), condition=%wide.region_2.3_spmd.clone, body=%wide.region_0.2_spmd.clone.sunk | while | flops 1075317248 | bytes 8401917 | solution.py:108
  304.3 3.3 fusion.80
  309.6 3.3 fusion.80
  314.8 3.3 fusion.80
  320.1 3.3 fusion.80
  330.6 3.3 fusion.80
  335.8 3.3 fusion.80
  341.1 3.3 fusion.80
  346.4 3.3 fusion.80
  367.4 3.3 fusion.80
  372.6 3.3 fusion.80
  377.9 3.3 fusion.80
  383.1 3.3 fusion.80
  387.2 4.2 %all-to-all-start = ((f32[8,2,512]{2,1,0:T(2,128)}), f32[8,2,512]{2,1,0:T(2,128)S(1)}, u32[]{:S(2)}, u32[]{:S(2)}) async-start(f32[8,2,512]{2,1,0:T(2,128)} %broadcast_in_dim.102), calls=%async_computation | async-start | bytes 65536 | tf_op jit(solution)/shard_map/all_to_all | solution.py:23
  391.3 5.1 %all-to-all-done = f32[8,2,512]{2,1,0:T(2,128)S(1)} async-done(((f32[8,2,512]{2,1,0:T(2,128)}), f32[8,2,512]{2,1,0:T(2,128)S(1)}, u32[]{:S(2)}, u32[]{:S(2)}) %all-to-all-start) | async-done | bytes 32800 | tf_op jit(solution)/shard_map/all_to_all | solution.py:23
  396.7 12.6 %all_to_all.10 = f32[16,2,4]{2,1,0:T(2,128)S(1)} all-to-all(f32[16,2,4]{2,1,0:T(2,128)S(1)} %broadcast_in_dim.103), channel_id=1, replica_groups=mesh['row'=4,'col'=2,'ex'=16] {'ex'}, dimensions={0} | all-to-all | bytes 1024 | tf_op jit(solution)/shard_map/all_to_all | solution.py:23
  (107 shorter events, 62.1 us)
Async XLA Ops:
  7.2 4.2 %copy-start = (f32[64,64]{1,0:T(8,128)S(1)}, f32[64,64]{1,0:T(8,128)}, u32[]{:S(2)}) copy-start(f32[64,64]{1,0:T(8,128)} %param.20) | copy-start | bytes 49156
  7.2 71.2 %all-gather.4.cloned.1.call-start = ((), (), s32[]{:S(2)}) async-start(), calls=%async_computation.2 | async-start | bytes 6823936 | tf_op jit(solution)/shard_map/all_gather | solution.py:16
  9.8 292.7 %all-gather.6.cloned.1.call-start = ((), (), s32[]{:S(2)}) async-start(), calls=%async_computation.3 | async-start | bytes 35651584 | tf_op jit(solution)/shard_map/all_gather | solution.py:94
  91.4 1.6 slice-start
  116.6 6.7 %copy-start.2 = (bf16[512,2048]{1,0:T(8,128)(2,1)S(1)}, bf16[512,2048]{1,0:T(8,128)(2,1)}, u32[]{:S(2)}) copy-start(bf16[512,2048]{1,0:T(8,128)(2,1)} %param.13) | copy-start | bytes 6291460
  123.4 2.5 copy-start.4
  386.5 23.4 %copy-start.1 = (f32[64,64]{1,0:T(8,128)S(1)}, f32[64,64]{1,0:T(8,128)}, u32[]{:S(2)}) copy-start(f32[64,64]{1,0:T(8,128)} %param.20) | copy-start | bytes 49156
  387.2 9.3 %all-to-all-start = ((f32[8,2,512]{2,1,0:T(2,128)}), f32[8,2,512]{2,1,0:T(2,128)S(1)}, u32[]{:S(2)}, u32[]{:S(2)}) async-start(f32[8,2,512]{2,1,0:T(2,128)} %broadcast_in_dim.102), calls=%async_computation | async-start | bytes 65536 | tf_op jit(solution)/shard_map/all_to_all | solution.py:23
  396.5 13.5 %copy-start.3 = (f32[2,512]{1,0:T(2,128)}, f32[2,512]{1,0:T(2,128)S(1)}, u32[]{:S(2)}) copy-start(f32[2,512]{1,0:T(2,128)S(1)} %reduce_sum.35) | copy-start | bytes 12292
Sparse Core Ops, SparseCore 0:
  10.4 67.9 all-gather.3
  116.7 185.6 all-gather.5
where the time goes:
time: 418 us; the launch traced here: 417 us
  waiting for transfers between devices  248 us (59%)
  matrix products  73.6 us (18%)
  local copies, waits for them, and re-layouts  56.6 us (14%)
  between operations  14.2 us (3%)
  blocking collectives  12.6 us (3%)
  other arithmetic  6.94 us (2%)
  starting transfers between devices  4.25 us (1%)
    all_gather x1, waiting for transfers between devices, body(): piece = lax.all_gather(precond, 'ex', axis=0, tiled=True)  176 us
    all_gather x1, waiting for transfers between devices, sent_together(): whole = lax.all_gather(both, axis, axis=dim, tiled=True)  66.4 us
    dot_general x16, matrix products, score_one(): lax.dot_general(acts, matrix, (((1,), (1,)), ((), ())), preferred_element...  52.8 us
    dynamic_slice x32, local copies, waits for them, and re-layouts, score_one(): lax.dynamic_index_in_dim(out_split, pair // in_sub, 1, keepdims=False)  29.2 us
    unnamed x14, local copies, waits for them, and re-layouts  18.3 us
    all_to_all x1, blocking collectives, sent_to_all(): lax.all_to_all(jnp.broadcast_to(shard[None], (size, *shard.shape)), axis,...  12.6 us
  transfers between devices with their start and end apart: 3, of which 3 were waited for; matrix products, arithmetic and copies ran while one was open for 3% of the time, Pallas kernels for 0%

commit v1 on v0

--- a/solution.py
+++ b/solution.py
@@ -6,6 +6,10 @@
 
 QUERIES = 2
 DAMPING = 0.1
+region_map = lambda mesh_dim, sample, dim_k: jnp.concatenate(
+    lax.all_to_all(jnp.stack([sample] * lax.axis_size(mesh_dim), axis=0), mesh_dim, 0, 0),
+    axis=dim_k,
+)
 
 
 def sent_together(arrays, axis, dim, along):
@@ -91,7 +95,7 @@
     in_split = train_in.reshape(tokens, in_sub, width)
     out_split = train_out.reshape(tokens, out_sub, width)
     query_range = jnp.arange(QUERIES, dtype=jnp.int32)
-    piece = lax.all_gather(precond, "ex", axis=0, tiled=True)
+    piece = region_map("ex", precond, 0)
 
     def score_one(step, running):
         pair = step // QUERIES

time: 418 us -> 806 us (1.93)
  waiting for transfers between devices: 248 us -> 611 us
  local copies, waits for them, and re-layouts: 56.6 us -> 67.6 us
    all_to_all x0 -> x1, waiting for transfers between devices: none -> 539 us  [lax.all_to_all(jnp.stack([sample] * lax.axis_size(mesh_dim), axis=0), mes...]
    all_gather x1 -> x0, waiting for transfers between devices: 176 us -> none  [body(): piece = lax.all_gather(precond, 'ex', axis=0, tiled=True)]
    another operation x0 -> x1, local copies, waits for them, and re-layouts: none -> 11.1 us  [jnp.stack([sample] * lax.axis_size(mesh_dim), axis=0)]
  transfers between devices with their start and end apart: 3 -> 3, of which waited for: 3 -> 3; matrix products, arithmetic and copies ran while one was open for 3% -> 1% of each run, Pallas kernels for 0% -> 0%
where the time goes in v1:
time: 806 us; the launch traced here: 804 us
  waiting for transfers between devices  611 us (76%)
  matrix products  74.3 us (9%)
  local copies, waits for them, and re-layouts  67.6 us (8%)
  blocking collectives  19.1 us (2%)
  between operations  14.2 us (2%)
  starting transfers between devices  10.3 us (1%)
    all_to_all x1, waiting for transfers between devices, lax.all_to_all(jnp.stack([sample] * lax.axis_size(mesh_dim), axis=0), mes...  539 us
    all_gather x1, waiting for transfers between devices, sent_together(): whole = lax.all_gather(both, axis, axis=dim, tiled=True)  66.5 us
    dot_general x16, matrix products, score_one(): lax.dot_general(acts, matrix, (((1,), (1,)), ((), ())), preferred_element...  52.8 us
    dynamic_slice x32, local copies, waits for them, and re-layouts, score_one(): lax.dynamic_index_in_dim(out_split, pair // in_sub, 1, keepdims=False)  29.2 us
    all_to_all x1, blocking collectives, sent_to_all(): lax.all_to_all(jnp.broadcast_to(shard[None], (size, *shard.shape)), axis,...  19.1 us
    unnamed x14, local copies, waits for them, and re-layouts  18.3 us
  transfers between devices with their start and end apart: 3, of which 3 were waited for; matrix products, arithmetic and copies ran while one was open for 1% of the time, Pallas kernels for 0%

profile of v1, /device:TPU:1, one launch (start us, length us, event | category | flops | bytes accessed | tf_op | source)
XLA Modules:
  0.0 804.0 jit_solution(17859401809099584376)
XLA Ops:
  11.9 66.5 %all-gather.2.cloned.1.call-done = bf16[512,6145]{1,0:T(8,128)(2,1)} async-done(((bf16[32,6145]{1,0:T(8,128)(2,1)}), bf16[512,6145]{1,0:T(8,128)(2,1)}) %all-gather.2.cloned.1.call-update) | async-done | bytes 6292496 | tf_op jit(solution)/shard_map/all_gather | solution.py:20
  78.3 4.7 split.12
  83.1 6.5 copy.58
  96.6 5.5 fusion.17
  102.1 3.9 fusion.13
  106.0 3.8 divide_convert_fusion
  109.9 7.4 fusion.22
  117.3 11.1 %stack.2 = bf16[16,1,1024,1024]{3,2,1,0:T(8,128)(2,1)} broadcast(bf16[1024,1024]{1,0:T(8,128)(2,1)S(1)} %fusion.22), dimensions={2,3} | broadcast | bytes 35651584 | tf_op jit(solution)/shard_map/stack | solution.py:10
  128.4 6.1 all-to-all-start
  134.5 6.7 copy.49
  143.9 539.4 %all-to-all-done = bf16[16,1,1024,1024]{3,2,1,0:T(8,128)(2,1)} async-done(((bf16[16,1,1024,1024]{3,2,1,0:T(8,128)(2,1)}), bf16[16,1,1024,1024]{3,2,1,0:T(8,128)(2,1)}, u32[]{:S(2)}, u32[]{:S(2)}) %all-to-all-start) | async-done | bytes 33554464 | tf_op jit(solution)/shard_map/all_to_all | solution.py:10
  683.3 84.1 %while.23 = (s32[]{:T(128)}, f32[2,512]{1,0:T(2,128)S(1)}, bf16[512,2,1024]{0,2,1:T(8,128)(2,1)}, bf16[16,1024,1024]{2,1,0:T(8,128)(2,1)}, bf16[512,4,1024]{0,2,...) while((s32[]{:T(128)}, f32[2,512]{1,0:T(2,128)S(1)}, ...), condition=%wide.region_2.3_spmd.clone, body=%wide.region_0.2_spmd.clone.sunk | while | flops 1075317248 | bytes 8401917 | solution.py:112
  685.1 3.3 fusion.80
  690.4 3.3 fusion.80
  695.6 3.3 fusion.80
  700.9 3.3 fusion.80
  716.7 3.3 fusion.80
  721.9 3.3 fusion.80
  727.2 3.3 fusion.80
  732.4 3.3 fusion.80
  748.2 3.3 fusion.80
  768.0 4.2 all-to-all-start.1
  772.2 5.1 all-to-all-done.1
  777.5 19.1 %all_to_all.15 = f32[16,2,4]{2,1,0:T(2,128)S(1)} all-to-all(f32[16,2,4]{2,1,0:T(2,128)S(1)} %broadcast_in_dim.103), channel_id=1, replica_groups=mesh['row'=4,'col'=2,'ex'=16] {'ex'}, dimensions={0} | all-to-all | bytes 1024 | tf_op jit(solution)/shard_map/all_to_all | solution.py:27
  (107 shorter events, 69.5 us)
Async XLA Ops:
  7.2 4.1 copy-start
  7.2 71.2 %all-gather.2.cloned.1.call-start = ((), (), s32[]{:S(2)}) async-start(), calls=%async_computation.3 | async-start | bytes 6823936 | tf_op jit(solution)/shard_map/all_gather | solution.py:20
  91.4 1.6 slice-start
  128.4 554.9 %all-to-all-start = ((bf16[16,1,1024,1024]{3,2,1,0:T(8,128)(2,1)}), bf16[16,1,1024,1024]{3,2,1,0:T(8,128)(2,1)}, u32[]{:S(2)}, u32[]{:S(2)}) async-start(bf16[16,1,1024,1024]{3,2,1,0:T(8,128)(2,1)} %stack.2), calls=%async_computation | async-start | bytes 67108864 | tf_op jit(solution)/shard_map/all_to_all | solution.py:10
  134.5 6.7 copy-start.2
  141.2 2.5 copy-start.4
  767.4 29.8 %copy-start.1 = (f32[64,64]{1,0:T(8,128)S(1)}, f32[64,64]{1,0:T(8,128)}, u32[]{:S(2)}) copy-start(f32[64,64]{1,0:T(8,128)} %param.20) | copy-start | bytes 49156
  768.0 9.3 %all-to-all-start.1 = ((f32[8,2,512]{2,1,0:T(2,128)}), f32[8,2,512]{2,1,0:T(2,128)S(1)}, u32[]{:S(2)}, u32[]{:S(2)}) async-start(f32[8,2,512]{2,1,0:T(2,128)} %broadcast_in_dim.102), calls=%async_computation.1 | async-start | bytes 65536 | tf_op jit(solution)/shard_map/all_to_all | solution.py:27
  777.3 19.9 %copy-start.3 = (f32[2,512]{1,0:T(2,128)}, f32[2,512]{1,0:T(2,128)S(1)}, u32[]{:S(2)}) copy-start(f32[2,512]{1,0:T(2,128)S(1)} %reduce_sum.35) | copy-start | bytes 12292
Sparse Core Ops, SparseCore 0:
  10.4 67.9 all-gather.1
